TPU v7x, 32 devices: a whole 2x2x4 slice. The times are simulated.
32 devices in a mesh: row: 4 (over z), col: 4 (over x, core), depth: 2 (over y).
Axes of the slice: x: 2, y: 2, z: 4, core: 2. Of those that a mesh axis runs over, the one named last changes fastest.
Arguments:
- heads_concat: bfloat16 [2048, 16384], P('row', ('depth', 'col')), may hold values from -6 to 6
- w_out: bfloat16 [16384, 7168], P(('depth', 'row'), 'col'), may hold values from -0.046875 to 0.046875
Outputs:
- projected: bfloat16 [2048, 7168], P('row', ('col', 'depth'))
All inputs are finite; a program needn't handle non-finite values.
Results may differ from a plain program's by a relative error of at most 0.001.
Values may be sent and summed in bfloat16 or wider, within the bound.
A program may use at most 128 MiB of HBM per device.

v0:
```python
import jax
import jax.numpy as jnp
from jax import lax
from jax.sharding import PartitionSpec as P


def per_device(heads_concat, w_out):
    head_half = lax.all_gather(heads_concat, "col", axis=1, tiled=True)
    weight_half = lax.all_gather(w_out, "row", axis=0, tiled=True)
    partial_sum = jnp.dot(head_half, weight_half, preferred_element_type=jnp.float32)
    summed = lax.psum_scatter(partial_sum, "depth", scatter_dimension=1, tiled=True)
    return summed.astype(jnp.bfloat16)


def solution(mesh):
    return jax.shard_map(
        per_device,
        mesh=mesh,
        in_specs=(P("row", ("depth", "col")), P(("depth", "row"), "col")),
        out_specs=P("row", ("col", "depth")),
        check_vma=False,
    )
```

profile of v0, /device:TPU:0, one launch (start us, length us, event | category | flops | bytes accessed | tf_op | source)
XLA Modules:
  0.0 643.9 jit_solution(13111015978111093550)
XLA Ops:
  6.5 0.0 all-gather.3.cloned.1.call-start
  6.5 0.7 all-gather.3.cloned.1.call-update
  7.3 0.0 all-gather.5.cloned.1.call-start
  7.3 0.7 all-gather.5.cloned.1.call-update
  8.0 0.0 reduce-scatter.2.cloned.1.call-start
  8.1 61.9 %all-gather.3.cloned.1.call-done = bf16[512,8192]{1,0:T(8,128)(2,1)} async-done(((bf16[512,2048]{1,0:T(8,128)(2,1)}), bf16[512,8192]{1,0:T(8,128)(2,1)}) %all-gather.3.cloned.1.call-update) | async-done | bytes 8388624 | tf_op jit(solution)/shard_map/all_gather | solution.py:8
  69.9 494.7 %all-gather.5.cloned.1.call-done = bf16[8192,1792]{1,0:T(8,128)(2,1)} async-done(((bf16[2048,1792]{1,0:T(8,128)(2,1)}), bf16[8192,1792]{1,0:T(8,128)(2,1)}) %all-gather.5.cloned.1.call-update) | async-done | bytes 29360144 | tf_op jit(solution)/shard_map/all_gather | solution.py:9
  564.6 22.7 %fusion = f32[512,1792]{1,0:T(8,128)} fusion(bf16[512,8192]{1,0:T(8,128)(2,1)} %all-gather.3.cloned.1.call-done, bf16[8192,1792]{1,0:T(8,128)(2,1)} %all-gather.5.cloned.1.call-done), kind=kOutput, calls=%fused_computation | convolution fusion | flops 15032385536 | bytes 41418752 | tf_op jit(solution)/shard_map/dot_general | solution.py:10
  587.3 0.0 reduce-scatter.2.cloned.1.call-update
  587.3 47.5 %reduce-scatter.2.cloned.1.call-done = f32[512,896]{1,0:T(8,128)} async-done(((f32[512,1792]{1,0:T(8,128)}), f32[512,896]{1,0:T(8,128)}) %reduce-scatter.2.cloned.1.call-update) | async-done | bytes 1835024 | tf_op jit(solution)/shard_map/reduce_scatter | solution.py:11
  634.9 2.5 convert_element_type.3
Async XLA Ops:
  6.5 63.4 %all-gather.3.cloned.1.call-start = ((), (), s32[]{:S(2)}) async-start(), calls=%async_computation.1 | async-start | bytes 10485760 | tf_op jit(solution)/shard_map/all_gather | solution.py:8
  7.3 557.4 %all-gather.5.cloned.1.call-start = ((), (), s32[]{:S(2)}) async-start(), calls=%async_computation.2 | async-start | bytes 36700160 | tf_op jit(solution)/shard_map/all_gather | solution.py:9
  8.0 626.9 %reduce-scatter.2.cloned.1.call-start = ((), (), s32[]{:S(2)}) async-start(), calls=%async_computation.3 | async-start | bytes 5505024 | tf_op jit(solution)/shard_map/reduce_scatter | solution.py:11
Sparse Core Ops, SparseCore 0:
  8.9 60.9 all-gather.2
  71.5 493.0 all-gather.4
  587.4 47.3 reduce-scatter.1
where the time goes:
time: 644 us
  waiting for transfers between devices  606 us (94%)
  matrix products  22.7 us (4%)
  between operations  13.1 us (2%)
    all_gather x1, waiting for transfers between devices, per_device(): weight_half = lax.all_gather(w_out, 'row', axis=0, tiled=True)  495 us
    all_gather x1, waiting for transfers between devices, per_device(): head_half = lax.all_gather(heads_concat, 'col', axis=1, tiled=True)  61.9 us
    reduce_scatter x1, waiting for transfers between devices, per_device(): lax.psum_scatter(partial_sum, 'depth', scatter_dimension=1, tiled=True)  47.5 us
    dot_general x1, matrix products, per_device(): jnp.dot(head_half, weight_half, preferred_element_type=jnp.float32)  22.7 us
  transfers between devices with their start and end apart: 3, of which 3 were waited for; matrix products, arithmetic and copies ran while one was open for 0% of the time, Pallas kernels for 0%

commit v1 on v0

--- a/solution.py
+++ b/solution.py
@@ -5,7 +5,7 @@
 
 
 def per_device(heads_concat, w_out):
-    head_half = lax.all_gather(heads_concat, "col", axis=1, tiled=True)
+    head_half = jnp.concatenate(lax.all_gather(heads_concat, "col"), axis=1)
     weight_half = lax.all_gather(w_out, "row", axis=0, tiled=True)
     partial_sum = jnp.dot(head_half, weight_half, preferred_element_type=jnp.float32)
     summed = lax.psum_scatter(partial_sum, "depth", scatter_dimension=1, tiled=True)

time: 644 us -> 645 us (level)
  waiting for transfers between devices: 606 us -> 594 us
  local copies, waits for them, and re-layouts: 0 us -> 11.7 us
    all_gather x1, waiting for transfers between devices: 495 us -> 483 us  [per_device(): weight_half = lax.all_gather(w_out, 'row', axis=0, tiled=True)]
    reshape x0 -> x1, local copies, waits for them, and re-layouts: none -> 11.7 us  [per_device(): head_half = jnp.concatenate(lax.all_gather(heads_concat, 'col'), axis=1)]
  transfers between devices with their start and end apart: 3 -> 3, of which waited for: 3 -> 3; matrix products, arithmetic and copies ran while one was open for 0% -> 2% of each run, Pallas kernels for 0% -> 0%
where the time goes in v1:
time: 645 us; the launch traced here: 644 us
  waiting for transfers between devices  594 us (92%)
  matrix products  22.9 us (4%)
  between operations  13.1 us (2%)
  local copies, waits for them, and re-layouts  11.7 us (2%)
    all_gather x1, waiting for transfers between devices, per_device(): weight_half = lax.all_gather(w_out, 'row', axis=0, tiled=True)  483 us
    all_gather x1, waiting for transfers between devices, per_device(): head_half = jnp.concatenate(lax.all_gather(heads_concat, 'col'), axis=1)  61.9 us
    reduce_scatter x1, waiting for transfers between devices, per_device(): lax.psum_scatter(partial_sum, 'depth', scatter_dimension=1, tiled=True)  47.5 us
    dot_general x1, matrix products, per_device(): jnp.dot(head_half, weight_half, preferred_element_type=jnp.float32)  22.9 us
  transfers between devices with their start and end apart: 3, of which 3 were waited for; matrix products, arithmetic and copies ran while one was open for 2% of the time, Pallas kernels for 0%

profile of v1, /device:TPU:0, one launch (start us, length us, event | category | flops | bytes accessed | tf_op | source)
XLA Modules:
  0.0 644.1 jit_solution(17387813092183159589)
XLA Ops:
  6.5 0.0 all-gather.6.cloned.1.call-start
  6.5 0.7 all-gather.6.cloned.1.call-update
  7.3 0.0 all-gather.4.cloned.1.call-start
  7.3 0.7 all-gather.4.cloned.1.call-update
  8.0 0.0 reduce-scatter.2.cloned.1.call-start
  8.1 61.9 %all-gather.6.cloned.1.call-done = bf16[2048,2048]{1,0:T(8,128)(2,1)} async-done(((bf16[512,2048]{1,0:T(8,128)(2,1)}), bf16[2048,2048]{1,0:T(8,128)(2,1)}) %all-gather.6.cloned.1.call-update) | async-done | bytes 8388624 | tf_op jit(solution)/shard_map/all_gather | solution.py:8
  69.9 11.7 %copy.3 = bf16[512,4,2048]{0,2,1:T(8,128)(2,1)} copy(bf16[512,4,2048]{2,0,1:T(8,128)(2,1)} %bitcast.6) | data formatting | bytes 16777216 | tf_op jit(solution)/shard_map/reshape | solution.py:8
  81.6 483.0 %all-gather.4.cloned.1.call-done = bf16[8192,1792]{1,0:T(8,128)(2,1)} async-done(((bf16[2048,1792]{1,0:T(8,128)(2,1)}), bf16[8192,1792]{1,0:T(8,128)(2,1)}) %all-gather.4.cloned.1.call-update) | async-done | bytes 29360144 | tf_op jit(solution)/shard_map/all_gather | solution.py:9
  564.6 22.9 %fusion = f32[512,1792]{1,0:T(8,128)} fusion(bf16[512,8192]{0,1:T(8,128)(2,1)} %bitcast.7, bf16[8192,1792]{1,0:T(8,128)(2,1)} %all-gather.4.cloned.1.call-done), kind=kOutput, calls=%fused_computation | convolution fusion | flops 15032385536 | bytes 41418752 | tf_op jit(solution)/shard_map/dot_general | solution.py:10
  587.5 0.0 reduce-scatter.2.cloned.1.call-update
  587.5 47.5 %reduce-scatter.2.cloned.1.call-done = f32[512,896]{1,0:T(8,128)} async-done(((f32[512,1792]{1,0:T(8,128)}), f32[512,896]{1,0:T(8,128)}) %reduce-scatter.2.cloned.1.call-update) | async-done | bytes 1835024 | tf_op jit(solution)/shard_map/reduce_scatter | solution.py:11
  635.1 2.5 convert_element_type.3
Async XLA Ops:
  6.5 63.4 %all-gather.6.cloned.1.call-start = ((), (), s32[]{:S(2)}) async-start(), calls=%async_computation.3 | async-start | bytes 10485760 | tf_op jit(solution)/shard_map/all_gather | solution.py:8
  7.3 557.4 %all-gather.4.cloned.1.call-start = ((), (), s32[]{:S(2)}) async-start(), calls=%async_computation.1 | async-start | bytes 36700160 | tf_op jit(solution)/shard_map/all_gather | solution.py:9
  8.0 627.1 %reduce-scatter.2.cloned.1.call-start = ((), (), s32[]{:S(2)}) async-start(), calls=%async_computation.2 | async-start | bytes 5505024 | tf_op jit(solution)/shard_map/reduce_scatter | solution.py:11
Sparse Core Ops, SparseCore 0:
  8.9 60.9 all-gather.5
  71.5 493.0 all-gather.3
  587.7 47.3 reduce-scatter.1
